TPU v7x, 128 devices: a whole 4x4x4 slice. The times are simulated.
128 devices in a mesh: dp: 16 (over x_lo, z, core), expert: 8 (over y, x_hi).
Axes of the slice: x: 4 (x_hi: 2, x_lo: 2; x = x_hi * 2 + x_lo), y: 4, z: 4, core: 2. Of those that a mesh axis runs over, the one named last changes fastest.
Arguments:
- tokens: bfloat16 [16384, 2048], P(('dp', 'expert')), may hold values from -6 to 6
- norm_gain: float32 [2048], replicated, may hold values from 0.25 to 1.75
- router_weight: bfloat16 [2048, 64], P('dp'), may hold values from -0.25 to 0.25
- expert_ids: int32 [16384, 8], P(('dp', 'expert')), may hold values from 0 to 63, all different within a row; in each aligned block of 128 rows (0 to 127, 128 to 255, ...) at most 32 rows name the same one
- gate_weight: bfloat16 [8, 2048, 1024], P('expert', 'dp'), may hold values from -0.125 to 0.125
- up_weight: bfloat16 [8, 2048, 1024], P('expert', 'dp'), may hold values from -0.125 to 0.125
- down_weight: bfloat16 [8, 2048, 1024], P('expert', 'dp'), may hold values from -0.1875 to 0.1875
- cotangent: bfloat16 [16384, 2048], P(('dp', 'expert')), may hold values from -6 to 6
Outputs:
- mixed: bfloat16 [16384, 2048], P(('dp', 'expert'))
- d_tokens: bfloat16 [16384, 2048], P(('dp', 'expert'))
- d_gain: float32 [2048], replicated
- d_router: float32 [2048, 64], P('dp')
- d_gate: bfloat16 [8, 2048, 1024], P('expert', 'dp')
- d_up: bfloat16 [8, 2048, 1024], P('expert', 'dp')
- d_down: bfloat16 [8, 2048, 1024], P('expert', 'dp')
Inputs may be any that keep to these rules, and one draw needn't show every extreme that they name: `expert_ids`: each row names 8 different experts; in the rows of one device no expert is named more than 32 times.
All inputs are finite; a program needn't handle non-finite values.
Results may differ from a plain program's by a relative error of at most 0.018.
Values may be sent and summed in bfloat16 or wider, within the bound.
No kernel may reach another device: no remote copies, remote signals or barrier semaphores. Data moves between devices by JAX's collectives and lax.ppermute only.
A program may use at most 128 MiB of HBM per device.

v0:
```python
import jax
import jax.numpy as jnp
from jax import lax
from jax.sharding import PartitionSpec as P

D = 2048
FF = 1024
CAP = 32
EPSILON = 1e-05
HIGHEST = lax.Precision.HIGHEST


def in_one_piece(arrays, axis, dim, along):
    both = jnp.concatenate(arrays, axis=along)
    result, at, finished = (lax.all_gather(both, axis, axis=dim, tiled=True), 0, [])
    for a in arrays:
        finished.append(lax.slice_in_dim(result, at, at + a.shape[along], axis=along))
        at += a.shape[along]
    return tuple(finished)


def split_up(x, dim, length):
    shape = x.shape
    pieces = x.reshape(*shape[:dim], length, shape[dim] // length, *shape[dim + 1 :])
    return jnp.moveaxis(pieces, dim, 0)


def sum_at_owner(x, axis, dim):
    length = lax.axis_size(axis)
    pieces = lax.all_to_all(split_up(x, dim, length), axis, 0, 0, tiled=True)
    return jnp.sum(pieces.astype(jnp.float32), axis=0)


def copy_for_each(x, axis):
    copies = jnp.broadcast_to(x, (lax.axis_size(axis), *x.shape))
    return lax.all_to_all(copies, axis, split_axis=0, concat_axis=0, tiled=True)


def over_copies(x, axis):
    everything = copy_for_each(x, axis)
    return jnp.sum(everything.astype(jnp.float32), axis=0)


def normalize(inputs, norm_gain):
    meansq = jnp.mean(inputs * inputs, axis=-1, keepdims=True)
    return inputs * lax.rsqrt(meansq + EPSILON) * norm_gain


def gate_weights(logits, expert_ids):
    member = (
        expert_ids[:, :, None] == jnp.arange(logits.shape[-1], dtype=jnp.int32)[None, None, :]
    ).astype(jnp.float32)
    picked = jnp.sum(member * logits[:, None, :], axis=-1)
    raised = jnp.exp(picked)
    return raised / jnp.sum(raised, axis=-1, keepdims=True)


def pick_matrix(expert_ids, window, capacity):
    flat_ids = expert_ids.reshape(-1)
    chosen = (flat_ids[:, None] == jnp.arange(window, dtype=jnp.int32)[None, :]).astype(jnp.int32)
    before = jnp.cumsum(chosen, axis=0, dtype=jnp.int32) - chosen
    position = jnp.sum(before * chosen, axis=-1)
    target = jnp.where(flat_ids < window, flat_ids * capacity + position, -1)
    columns = jnp.arange(window * capacity, dtype=jnp.int32)
    matrix = (target[:, None] == columns[None, :]).astype(jnp.float32)
    return matrix.reshape(expert_ids.shape[0], expert_ids.shape[1], window * capacity)


def expert_forward(slot_rows, w_gate, w_up, w_down):
    gate_pre = jnp.dot(slot_rows, w_gate, preferred_element_type=jnp.float32)
    up_pre = jnp.dot(slot_rows, w_up, preferred_element_type=jnp.float32)
    active = (gate_pre * jax.nn.sigmoid(gate_pre) * up_pre).astype(jnp.bfloat16)
    output = jnp.dot(active, w_down.T, preferred_element_type=jnp.float32).astype(jnp.bfloat16)
    return (output, gate_pre, up_pre)


def expert_backward(slot_grads, gate_pre, up_pre, w_gate, w_up, w_down):
    sigmoid_gate = jax.nn.sigmoid(gate_pre)
    active = (gate_pre * sigmoid_gate * up_pre).astype(jnp.bfloat16)
    back = jnp.dot(slot_grads, w_down, preferred_element_type=jnp.float32)
    grad_gate = (back * up_pre * sigmoid_gate * (1.0 + gate_pre * (1.0 - sigmoid_gate))).astype(
        jnp.bfloat16
    )
    grad_upper = (back * gate_pre * sigmoid_gate).astype(jnp.bfloat16)
    grad_rows = jnp.dot(grad_gate, w_gate.T, preferred_element_type=jnp.float32)
    grad_rows = (
        grad_rows + jnp.dot(grad_upper, w_up.T, preferred_element_type=jnp.float32)
    ).astype(jnp.bfloat16)
    return (grad_rows, active, grad_gate, grad_upper)


def body(
    tokens, norm_gain, router_weight, expert_ids, gate_weight, up_weight, down_weight, cotangent
):
    window = lax.axis_size("expert")
    slot_count = window * CAP
    router_full = lax.all_gather(router_weight, "dp", axis=0, tiled=True)
    inputs = tokens.astype(jnp.float32)
    hidden = normalize(inputs, norm_gain).astype(jnp.bfloat16)
    logits = jnp.dot(hidden, router_full, preferred_element_type=jnp.float32)
    weights, gate_back = jax.vjp(lambda values: gate_weights(values, expert_ids), logits)
    pick_table = pick_matrix(expert_ids, window, CAP)
    spread_half = jnp.sum(pick_table, axis=1).astype(jnp.bfloat16)
    blending = jnp.einsum("tks,tk->ts", pick_table, weights, precision=HIGHEST)
    outgoing = (
        jnp.dot(spread_half.T, hidden, preferred_element_type=jnp.float32)
        .astype(jnp.bfloat16)
        .reshape(window, CAP, D)
    )
    weights_full = in_one_piece((gate_weight, up_weight, down_weight), "dp", 1, 0)
    w_gate = weights_full[0][0]
    w_up = weights_full[1][0]
    w_down = weights_full[2][0]
    arrived_rows = lax.all_to_all(outgoing, "expert", split_axis=0, concat_axis=0, tiled=True)
    lead = arrived_rows.shape[0]
    middle = arrived_rows.shape[1]
    output, gate_pre, up_pre = expert_forward(arrived_rows.reshape(-1, D), w_gate, w_up, w_down)
    produced = output.reshape(lead, middle, D)
    gate_slots = gate_pre.reshape(lead, middle, FF)
    upper_slots = up_pre.reshape(lead, middle, FF)
    returned = lax.all_to_all(produced, "expert", split_axis=0, concat_axis=0, tiled=True).reshape(
        slot_count, D
    )
    returned_wide = returned.astype(jnp.float32)
    mixed_out = jnp.dot(blending, returned_wide, precision=HIGHEST).astype(jnp.bfloat16)
    gathered_cot = jnp.dot(spread_half.T, cotangent, preferred_element_type=jnp.float32)
    per_slot = jnp.sum(gathered_cot * returned_wide, axis=-1)
    grad_weights = jnp.einsum("tks,s->tk", pick_table, per_slot, precision=HIGHEST)
    grad_logits = gate_back(grad_weights)[0]
    outgoing_grad = (
        jnp.dot(blending.T, cotangent.astype(jnp.float32), precision=HIGHEST)
        .astype(jnp.bfloat16)
        .reshape(window, CAP, D)
    )
    arrived_grad = lax.all_to_all(outgoing_grad, "expert", split_axis=0, concat_axis=0, tiled=True)
    flat_rows = arrived_rows.reshape(-1, D)
    flat_grads = arrived_grad.reshape(-1, D)
    grad_rows, active, grad_gate, grad_upper = expert_backward(
        flat_grads, gate_slots.reshape(-1, FF), upper_slots.reshape(-1, FF), w_gate, w_up, w_down
    )
    grad_back = lax.all_to_all(
        grad_rows.reshape(window, CAP, D), "expert", split_axis=0, concat_axis=0, tiled=True
    ).reshape(slot_count, D)
    term_gate = jnp.dot(flat_rows.T, grad_gate, preferred_element_type=jnp.float32)
    term_upper = jnp.dot(flat_rows.T, grad_upper, preferred_element_type=jnp.float32)
    term_down = jnp.dot(flat_grads.T, active, preferred_element_type=jnp.float32)
    summed = lax.psum_scatter(
        jnp.concatenate([term_gate, term_upper, term_down], axis=1).astype(jnp.bfloat16),
        "dp",
        scatter_dimension=0,
        tiled=True,
    ).astype(jnp.float32)
    grad_hidden = jnp.dot(spread_half, grad_back, preferred_element_type=jnp.float32)
    grad_hidden = grad_hidden + jnp.dot(
        grad_logits, router_full.astype(jnp.float32).T, precision=HIGHEST
    )
    unused_value, norm_back = jax.vjp(normalize, inputs, norm_gain)
    grad_inputs, grad_gain = norm_back(grad_hidden)
    grad_router = jnp.dot(hidden.astype(jnp.float32).T, grad_logits, precision=HIGHEST)
    router_part = sum_at_owner(grad_router.astype(jnp.bfloat16), "dp", 0)
    router_mine = over_copies(router_part.astype(jnp.bfloat16), "expert").astype(jnp.float32)
    gain_sum = lax.psum(grad_gain, ("dp", "expert"))
    grad_gate_out = summed[:, :FF].astype(jnp.bfloat16)[None]
    grad_up_out = summed[:, FF : 2 * FF].astype(jnp.bfloat16)[None]
    grad_down_out = summed[:, 2 * FF :].astype(jnp.bfloat16)[None]
    return (
        mixed_out,
        grad_inputs.astype(jnp.bfloat16),
        gain_sum,
        router_mine,
        grad_gate_out,
        grad_up_out,
        grad_down_out,
    )


def solution(mesh):
    in_specs = (
        P(("dp", "expert"), None),
        P(),
        P("dp", None),
        P(("dp", "expert"), None),
        P("expert", "dp", None),
        P("expert", "dp", None),
        P("expert", "dp", None),
        P(("dp", "expert"), None),
    )
    out_specs = (
        P(("dp", "expert"), None),
        P(("dp", "expert"), None),
        P(),
        P("dp", None),
        P("expert", "dp", None),
        P("expert", "dp", None),
        P("expert", "dp", None),
    )
    return jax.shard_map(body, mesh=mesh, in_specs=in_specs, out_specs=out_specs, check_vma=False)
```

profile of v0, /device:TPU:1, one launch (start us, length us, event | category | flops | bytes accessed | tf_op | source)
XLA Modules:
  0.0 330.0 jit_solution(3319858266487233548)
XLA Ops:
  7.3 2.2 pad_maximum_fusion.1
  10.4 2.3 reduce-window.6
  15.9 2.5 convolution_convert_fusion.3
  18.4 7.5 %all-to-all-start = ((bf16[8,32,2048]{2,1,0:T(8,128)(2,1)}), bf16[8,32,2048]{2,1,0:T(8,128)(2,1)S(1)}, u32[]{:S(2)}, u32[]{:S(2)}) async-start(bf16[8,32,2048]{2,1,0:T(8,128)(2,1)} %bitcast.3), calls=%async_computation | async-start | bytes 2097152 | tf_op jit(solution)/shard_map/all_to_all | solution.py:114
  25.9 41.0 %all_gather.6 = bf16[2048,64]{0,1:T(8,128)(2,1)S(1)} all-gather(bf16[128,64]{0,1:T(8,128)(2,1)S(1)} %copy-done.14), channel_id=1, replica_groups=mesh['dp'=16,'expert'=8] {'dp'}, dimensions={0}, use_global_device_ids=true | all-gather | bytes 278528 | tf_op jit(solution)/shard_map/all_gather | solution.py:97
  71.1 6.8 %all-to-all-start.2 = ((bf16[8,32,2048]{2,1,0:T(8,128)(2,1)}), bf16[8,32,2048]{2,1,0:T(8,128)(2,1)S(1)}, u32[]{:S(2)}, u32[]{:S(2)}) async-start(bf16[8,32,2048]{2,1,0:T(8,128)(2,1)} %bitcast.109), calls=%async_computation.2 | async-start | bytes 2097152 | tf_op jit(solution)/shard_map/all_to_all | solution.py:135
  78.1 30.4 %all-gather.2.cloned.1.call-done = bf16[3,2048,1024]{2,1,0:T(8,128)(2,1)} async-done(((bf16[3,128,1024]{2,1,0:T(8,128)(2,1)}), bf16[3,2048,1024]{2,1,0:T(8,128)(2,1)}) %all-gather.2.cloned.1.call-update) | async-done | bytes 12582928 | tf_op jit(solution)/shard_map/all_gather | solution.py:15
  108.5 4.4 %fusion.3 = f32[256,1024]{1,0:T(8,128)} fusion(bf16[256,2048]{1,0:T(8,128)(2,1)S(1)} %bitcast.100, bf16[3,2048,1024]{2,1,0:T(8,128)(2,1)} %all-gather.2.cloned.1.call-done), kind=kOutput, calls=%fused_computation.10 | convolution fusion | flops 1073741824 | bytes 6291456 | tf_op jit(solution)/shard_map/dot_general | solution.py:71
  112.9 4.4 %fusion.1 = f32[256,1024]{1,0:T(8,128)} fusion(bf16[256,2048]{1,0:T(8,128)(2,1)S(1)} %bitcast.101, bf16[3,2048,1024]{2,1,0:T(8,128)(2,1)} %all-gather.2.cloned.1.call-done), kind=kOutput, calls=%fused_computation.8 | convolution fusion | flops 1073741824 | bytes 6291456 | tf_op jit(solution)/shard_map/dot_general | solution.py:70
  117.3 4.4 %multiply_convert_fusion = (bf16[256,1024]{1,0:T(8,128)(2,1)S(1)}, bf16[256,1024]{1,0:T(8,128)(2,1)S(1)}, bf16[256,1024]{1,0:T(8,128)(2,1)S(1)}) fusion(f32[256,1024]{1,0:T(8,128)} %fusion.1, f32[256,1024]{1,0:T(8,128)} %fusion.3, bf16[256,2048]{1,0:T(8,128)(2,1)S(1)} %bitcast.104, bf16[3,2048,1024]{2,1,0:T(8,128)(2,1)} %all-gather.2.cloned.1.call-done), kind=kOutput, calls=%fused_computation.36 | convolution fusion | flops 1077936128 | bytes 8912896 | tf_op jit(solution)/shard_map/dot_general | solution.py:80
  125.7 21.2 %pad_maximum_fusion = bf16[2048,3072]{0,1:T(8,128)(2,1)} fusion(bf16[2048,1024]{0,1:T(8,128)(2,1)S(1)} %convolution_convert_fusion, bf16[2048,1024]{0,1:T(8,128)(2,1)S(1)} %convolution_convert_fusion.1, bf16[2048,1024]{0,1:T(8,128)(2,1)S(1)} %convolution_convert_fusion.2), kind=kLoop, calls=%fused_computation | loop fusion | flops 37748736 | bytes 25165824 | tf_op jit(solution)/shard_map/concatenate | solution.py:148
  146.9 16.6 %copy.68 = bf16[2048,3072]{1,0:T(8,128)(2,1)} copy(bf16[2048,3072]{0,1:T(8,128)(2,1)} %pad_maximum_fusion) | data formatting | bytes 25165824
  164.6 4.6 %fusion.8 = bf16[256,2048]{1,0:T(8,128)(2,1)} fusion(bf16[256,1024]{1,0:T(8,128)(2,1)S(1)} %copy-done.8, bf16[3,2048,1024]{2,1,0:T(8,128)(2,1)} %all-gather.2.cloned.1.call-done), kind=kOutput, calls=%fused_computation.17 | convolution fusion | flops 1074266112 | bytes 5767168 | tf_op jit(solution)/shard_map/dot_general | solution.py:73
  169.2 6.1 %all-to-all-start.1 = ((bf16[8,32,2048]{2,1,0:T(8,128)(2,1)}), bf16[8,32,2048]{2,1,0:T(8,128)(2,1)S(1)}, u32[]{:S(2)}, u32[]{:S(2)}) async-start(bf16[8,32,2048]{2,1,0:T(8,128)(2,1)} %bitcast.8), calls=%async_computation.1 | async-start | bytes 2097152 | tf_op jit(solution)/shard_map/all_to_all | solution.py:121
  175.3 3.5 %fusion = f32[256,2048]{1,0:T(8,128)S(1)} fusion(bf16[256,1024]{1,0:T(8,128)(2,1)S(1)} %copy-done.6, bf16[3,2048,1024]{2,1,0:T(8,128)(2,1)} %all-gather.2.cloned.1.call-done), kind=kOutput, calls=%fused_computation.7 | convolution fusion | flops 1073741824 | bytes 6815744 | tf_op jit(solution)/shard_map/dot_general | solution.py:85
  178.9 4.5 %fusion.7 = bf16[256,2048]{1,0:T(8,128)(2,1)} fusion(f32[256,2048]{1,0:T(8,128)S(1)} %fusion, bf16[256,1024]{1,0:T(8,128)(2,1)S(1)} %copy-done.4, bf16[3,2048,1024]{2,1,0:T(8,128)(2,1)} %all-gather.2.cloned.1.call-done), kind=kOutput, calls=%fused_computation.16 | convolution fusion | flops 1074790400 | bytes 7864320 | tf_op jit(solution)/shard_map/dot_general | solution.py:87
  183.4 14.9 %all-to-all-done.1 = bf16[8,32,2048]{2,1,0:T(8,128)(2,1)S(1)} async-done(((bf16[8,32,2048]{2,1,0:T(8,128)(2,1)}), bf16[8,32,2048]{2,1,0:T(8,128)(2,1)S(1)}, u32[]{:S(2)}, u32[]{:S(2)}) %all-to-all-start.1) | async-done | bytes 1048608 | tf_op jit(solution)/shard_map/all_to_all | solution.py:121
  198.3 3.6 %all-to-all-start.3 = ((bf16[8,32,2048]{2,1,0:T(8,128)(2,1)}), bf16[8,32,2048]{2,1,0:T(8,128)(2,1)S(1)}, u32[]{:S(2)}, u32[]{:S(2)}) async-start(bf16[8,32,2048]{2,1,0:T(8,128)(2,1)} %bitcast.110), calls=%async_computation.3 | async-start | bytes 2097152 | tf_op jit(solution)/shard_map/all_to_all | solution.py:141
  202.4 3.6 %fusion.18 = f32[1,128,8]{2,0,1:T(1,128)S(1)} fusion(f32[256,1,1]{0,1,2:T(1,128)S(1)} %bitcast.115, s32[128,8]{1,0:T(8,128)S(1)} %copy.59), kind=kOutput, calls=%fused_computation.42 | convolution fusion | flops 3407872 | bytes 9216 | tf_op jit(solution)/shard_map/tks,s->tk/dot_general | solution.py:128
  207.6 16.8 %all-to-all-done.3 = bf16[8,32,2048]{2,1,0:T(8,128)(2,1)S(1)} async-done(((bf16[8,32,2048]{2,1,0:T(8,128)(2,1)}), bf16[8,32,2048]{2,1,0:T(8,128)(2,1)S(1)}, u32[]{:S(2)}, u32[]{:S(2)}) %all-to-all-start.3) | async-done | bytes 1048608 | tf_op jit(solution)/shard_map/all_to_all | solution.py:141
  224.4 6.8 %all-to-all-start.4 = ((bf16[16,128,64]{1,2,0:T(8,128)(2,1)}), bf16[16,128,64]{1,2,0:T(8,128)(2,1)S(1)}, u32[]{:S(2)}, u32[]{:S(2)}) async-start(bf16[16,128,64]{1,2,0:T(8,128)(2,1)} %bitcast.98), calls=%async_computation.4 | async-start | bytes 524288 | tf_op jit(solution)/shard_map/all_to_all | solution.py:30
  235.2 5.1 %all-to-all-done.4 = bf16[16,128,64]{1,2,0:T(8,128)(2,1)S(1)} async-done(((bf16[16,128,64]{1,2,0:T(8,128)(2,1)}), bf16[16,128,64]{1,2,0:T(8,128)(2,1)S(1)}, u32[]{:S(2)}, u32[]{:S(2)}) %all-to-all-start.4) | async-done | bytes 262176 | tf_op jit(solution)/shard_map/all_to_all | solution.py:30
  241.0 3.4 %all-to-all-start.5 = ((bf16[8,128,64]{1,2,0:T(8,128)(2,1)}), bf16[8,128,64]{1,2,0:T(8,128)(2,1)S(1)}, u32[]{:S(2)}, u32[]{:S(2)}) async-start(bf16[8,128,64]{1,2,0:T(8,128)(2,1)} %broadcast_in_dim.44), calls=%async_computation.5 | async-start | bytes 262144 | tf_op jit(solution)/shard_map/all_to_all | solution.py:36
  245.8 72.5 %psum.7 = f32[2048]{0:T(1024)} all-reduce(f32[2048]{0:T(1024)S(1)} %get-tuple-element.42), channel_id=1, replica_groups=mesh['dp'=16,'expert'=8] {'dp','expert'}, use_global_device_ids=true, to_apply=%region_12.13 | all-reduce | flops 2048 | bytes 16384 | tf_op jit(solution)/shard_map/psum | solution.py:162
  (93 shorter events, 26.4 us)
Async XLA Ops:
  7.2 61.8 %copy-start = (bf16[128,2048]{1,0:T(8,128)(2,1)S(1)}, bf16[128,2048]{1,0:T(8,128)(2,1)}, u32[]{:S(2)}) copy-start(bf16[128,2048]{1,0:T(8,128)(2,1)} %param.15) | copy-start | bytes 1572868
  7.2 60.9 %copy-start.13 = (s32[128,8]{0,1:T(8,128)S(1)}, s32[128,8]{0,1:T(8,128)}, u32[]{:S(2)}) copy-start(s32[128,8]{0,1:T(8,128)} %param.11) | copy-start | bytes 12292
  7.2 60.5 %copy-start.1 = (bf16[128,2048]{1,0:T(8,128)(2,1)S(1)}, bf16[128,2048]{1,0:T(8,128)(2,1)}, u32[]{:S(2)}) copy-start(bf16[128,2048]{1,0:T(8,128)(2,1)} %param.8) | copy-start | bytes 1572868
  7.2 60.5 %copy-start.12 = (f32[2048]{0:T(1024)S(1)}, f32[2048]{0:T(1024)}, u32[]{:S(2)}) copy-start(f32[2048]{0:T(1024)} %param.9) | copy-start | bytes 24580
  7.2 18.7 %copy-start.14 = (bf16[128,64]{0,1:T(8,128)(2,1)S(1)}, bf16[128,64]{0,1:T(8,128)(2,1)}, u32[]{:S(2)}) copy-start(bf16[128,64]{0,1:T(8,128)(2,1)} %param.10) | copy-start | bytes 49156
  7.2 101.3 %all-gather.2.cloned.1.call-start = ((), (), s32[]{:S(2)}) async-start(), calls=%async_computation.7 | async-start | bytes 13369344 | tf_op jit(solution)/shard_map/all_gather | solution.py:15
  15.9 10.0 %copy-start.17 = (f32[128]{0:T(128)}, f32[128]{0:T(128)S(1)}, u32[]{:S(2)}) copy-start(f32[128]{0:T(128)S(1)} %fusion.16) | copy-start | bytes 1540
  15.9 190.3 %copy-start.15 = (f32[128]{0:T(128)}, f32[128]{0:T(128)S(1)}, u32[]{:S(2)}) copy-start(f32[128]{0:T(128)S(1)} %fusion.34) | copy-start | bytes 1540
  18.4 52.6 %all-to-all-start = ((bf16[8,32,2048]{2,1,0:T(8,128)(2,1)}), bf16[8,32,2048]{2,1,0:T(8,128)(2,1)S(1)}, u32[]{:S(2)}, u32[]{:S(2)}) async-start(bf16[8,32,2048]{2,1,0:T(8,128)(2,1)} %bitcast.3), calls=%async_computation | async-start | bytes 2097152 | tf_op jit(solution)/shard_map/all_to_all | solution.py:114
  69.0 2.1 copy-start.9
  71.1 46.3 %all-to-all-start.2 = ((bf16[8,32,2048]{2,1,0:T(8,128)(2,1)}), bf16[8,32,2048]{2,1,0:T(8,128)(2,1)S(1)}, u32[]{:S(2)}, u32[]{:S(2)}) async-start(bf16[8,32,2048]{2,1,0:T(8,128)(2,1)} %bitcast.109), calls=%async_computation.2 | async-start | bytes 2097152 | tf_op jit(solution)/shard_map/all_to_all | solution.py:135
  77.9 241.0 %reduce-scatter.4.cloned.1.call-start = ((), (), s32[]{:S(2)}) async-start(), calls=%async_computation.8 | async-start | bytes 13369344
  121.7 1.4 copy-start.7
  121.7 1.4 copy-start.3
  121.7 2.7 copy-start.5
  163.5 1.0 copy-start.8
  164.6 10.7 %copy-start.6 = (bf16[256,1024]{1,0:T(8,128)(2,1)S(1)}, bf16[256,1024]{1,0:T(8,128)(2,1)}, u32[]{:S(2)}) copy-start(bf16[256,1024]{1,0:T(8,128)(2,1)} %copy-done.5) | copy-start | bytes 1572868
  169.2 29.1 %all-to-all-start.1 = ((bf16[8,32,2048]{2,1,0:T(8,128)(2,1)}), bf16[8,32,2048]{2,1,0:T(8,128)(2,1)S(1)}, u32[]{:S(2)}, u32[]{:S(2)}) async-start(bf16[8,32,2048]{2,1,0:T(8,128)(2,1)} %bitcast.8), calls=%async_computation.1 | async-start | bytes 2097152 | tf_op jit(solution)/shard_map/all_to_all | solution.py:121
  175.3 3.5 %copy-start.4 = (bf16[256,1024]{1,0:T(8,128)(2,1)S(1)}, bf16[256,1024]{1,0:T(8,128)(2,1)}, u32[]{:S(2)}) copy-start(bf16[256,1024]{1,0:T(8,128)(2,1)} %copy-done.3) | copy-start | bytes 1572868
  198.3 26.1 %all-to-all-start.3 = ((bf16[8,32,2048]{2,1,0:T(8,128)(2,1)}), bf16[8,32,2048]{2,1,0:T(8,128)(2,1)S(1)}, u32[]{:S(2)}, u32[]{:S(2)}) async-start(bf16[8,32,2048]{2,1,0:T(8,128)(2,1)} %bitcast.110), calls=%async_computation.3 | async-start | bytes 2097152 | tf_op jit(solution)/shard_map/all_to_all | solution.py:141
  224.4 15.9 %all-to-all-start.4 = ((bf16[16,128,64]{1,2,0:T(8,128)(2,1)}), bf16[16,128,64]{1,2,0:T(8,128)(2,1)S(1)}, u32[]{:S(2)}, u32[]{:S(2)}) async-start(bf16[16,128,64]{1,2,0:T(8,128)(2,1)} %bitcast.98), calls=%async_computation.4 | async-start | bytes 524288 | tf_op jit(solution)/shard_map/all_to_all | solution.py:30
  231.2 2.9 copy-start.16
  231.5 12.9 %copy-start.10 = (f32[128,1,256]{2,1,0:T(1,128)S(1)}, f32[128,1,256]{2,1,0:T(1,128)}, u32[]{:S(2)}) copy-start(f32[128,1,256]{2,1,0:T(1,128)} %copy-done.9) | copy-start | bytes 393220
  241.0 77.3 %all-to-all-start.5 = ((bf16[8,128,64]{1,2,0:T(8,128)(2,1)}), bf16[8,128,64]{1,2,0:T(8,128)(2,1)S(1)}, u32[]{:S(2)}, u32[]{:S(2)}) async-start(bf16[8,128,64]{1,2,0:T(8,128)(2,1)} %broadcast_in_dim.44), calls=%async_computation.5 | async-start | bytes 262144 | tf_op jit(solution)/shard_map/all_to_all | solution.py:36
  (2 other events, 1.3 us)
Sparse Core Ops, SparseCore 0:
  9.7 98.7 all-gather.1
  163.7 106.8 reduce-scatter.3
where the time goes:
time: 331 us; the launch traced here: 330 us
  blocking collectives  114 us (34%)
  waiting for transfers between devices  67.2 us (20%)
  matrix products  43.8 us (13%)
  starting transfers between devices  34.4 us (10%)
  other arithmetic  30.8 us (9%)
  local copies, waits for them, and re-layouts  25.9 us (8%)
  between operations  14.4 us (4%)
    psum x1, blocking collectives, body(): gain_sum = lax.psum(grad_gain, ('dp', 'expert'))  72.5 us
    all_gather x1, blocking collectives, body(): router_full = lax.all_gather(router_weight, 'dp', axis=0, tiled=True)  41 us
    all_gather x1, waiting for transfers between devices, in_one_piece(): lax.all_gather(both, axis, axis=dim, tiled=True)  30.4 us
    unnamed x44, local copies, waits for them, and re-layouts  22.4 us
    concatenate x1, other arithmetic, body(): jnp.concatenate([term_gate, term_upper, term_down], axis=1)  21.2 us
    all_to_all x1, waiting for transfers between devices, body(): lax.all_to_all(grad_rows.reshape(window, CAP, D), 'expert', split_axis=0,...  16.8 us
    all_to_all x1, waiting for transfers between devices, body(): lax.all_to_all(produced, 'expert', split_axis=0, concat_axis=0, tiled=True)  14.9 us
    all_to_all x1, starting transfers between devices, body(): lax.all_to_all(outgoing, 'expert', split_axis=0, concat_axis=0, tiled=True)  7.46 us
  transfers between devices with their start and end apart: 8, of which 4 were waited for; matrix products, arithmetic and copies ran while one was open for 14% of the time, Pallas kernels for 0%

commit v1 on v0

--- a/solution.py
+++ b/solution.py
@@ -159,7 +159,9 @@
     grad_router = jnp.dot(hidden.astype(jnp.float32).T, grad_logits, precision=HIGHEST)
     router_part = sum_at_owner(grad_router.astype(jnp.bfloat16), "dp", 0)
     router_mine = over_copies(router_part.astype(jnp.bfloat16), "expert").astype(jnp.float32)
-    gain_sum = lax.psum(grad_gain, ("dp", "expert"))
+    gain_sum = grad_gain
+    for mesh_axis in ("expert", "dp"):
+        gain_sum = lax.psum(gain_sum, mesh_axis)
     grad_gate_out = summed[:, :FF].astype(jnp.bfloat16)[None]
     grad_up_out = summed[:, FF : 2 * FF].astype(jnp.bfloat16)[None]
     grad_down_out = summed[:, 2 * FF :].astype(jnp.bfloat16)[None]

time: 331 us -> 313 us (0.946)
  blocking collectives: 114 us -> 94.8 us
    psum x1 -> x2, blocking collectives: 72.5 us -> 53.8 us  [body(): gain_sum = lax.psum(gain_sum, mesh_axis)]
  transfers between devices with their start and end apart: 8 -> 8, of which waited for: 4 -> 4; matrix products, arithmetic and copies ran while one was open for 14% -> 15% of each run, Pallas kernels for 0% -> 0%
where the time goes in v1:
time: 313 us; the launch traced here: 311 us
  blocking collectives  94.8 us (30%)
  waiting for transfers between devices  67.2 us (21%)
  matrix products  43.8 us (14%)
  starting transfers between devices  34.4 us (11%)
  other arithmetic  30.8 us (10%)
  local copies, waits for them, and re-layouts  25.9 us (8%)
  between operations  14.4 us (5%)
    psum x2, blocking collectives, body(): gain_sum = lax.psum(gain_sum, mesh_axis)  53.8 us
    all_gather x1, blocking collectives, body(): router_full = lax.all_gather(router_weight, 'dp', axis=0, tiled=True)  41 us
    all_gather x1, waiting for transfers between devices, in_one_piece(): lax.all_gather(both, axis, axis=dim, tiled=True)  30.4 us
    unnamed x44, local copies, waits for them, and re-layouts  22.4 us
    concatenate x1, other arithmetic, body(): jnp.concatenate([term_gate, term_upper, term_down], axis=1)  21.2 us
    all_to_all x1, waiting for transfers between devices, body(): lax.all_to_all(grad_rows.reshape(window, CAP, D), 'expert', split_axis=0,...  16.8 us
    all_to_all x1, waiting for transfers between devices, body(): lax.all_to_all(produced, 'expert', split_axis=0, concat_axis=0, tiled=True)  14.9 us
    all_to_all x1, starting transfers between devices, body(): lax.all_to_all(outgoing, 'expert', split_axis=0, concat_axis=0, tiled=True)  7.46 us
  transfers between devices with their start and end apart: 8, of which 4 were waited for; matrix products, arithmetic and copies ran while one was open for 15% of the time, Pallas kernels for 0%

profile of v1, /device:TPU:1, one launch (start us, length us, event | category | flops | bytes accessed | tf_op | source)
XLA Modules:
  0.0 311.3 jit_solution(18027880678268970903)
XLA Ops:
  10.4 2.3 reduce-window.6
  15.9 2.5 convolution_convert_fusion.3
  18.4 7.5 %all-to-all-start = ((bf16[8,32,2048]{2,1,0:T(8,128)(2,1)}), bf16[8,32,2048]{2,1,0:T(8,128)(2,1)S(1)}, u32[]{:S(2)}, u32[]{:S(2)}) async-start(bf16[8,32,2048]{2,1,0:T(8,128)(2,1)} %bitcast.3), calls=%async_computation | async-start | bytes 2097152 | tf_op jit(solution)/shard_map/all_to_all | solution.py:114
  25.9 41.0 %all_gather.6 = bf16[2048,64]{0,1:T(8,128)(2,1)S(1)} all-gather(bf16[128,64]{0,1:T(8,128)(2,1)S(1)} %copy-done.14), channel_id=1, replica_groups=mesh['dp'=16,'expert'=8] {'dp'}, dimensions={0}, use_global_device_ids=true | all-gather | bytes 278528 | tf_op jit(solution)/shard_map/all_gather | solution.py:97
  71.1 6.8 %all-to-all-start.2 = ((bf16[8,32,2048]{2,1,0:T(8,128)(2,1)}), bf16[8,32,2048]{2,1,0:T(8,128)(2,1)S(1)}, u32[]{:S(2)}, u32[]{:S(2)}) async-start(bf16[8,32,2048]{2,1,0:T(8,128)(2,1)} %bitcast.109), calls=%async_computation.2 | async-start | bytes 2097152 | tf_op jit(solution)/shard_map/all_to_all | solution.py:135
  78.1 30.4 %all-gather.2.cloned.1.call-done = bf16[3,2048,1024]{2,1,0:T(8,128)(2,1)} async-done(((bf16[3,128,1024]{2,1,0:T(8,128)(2,1)}), bf16[3,2048,1024]{2,1,0:T(8,128)(2,1)}) %all-gather.2.cloned.1.call-update) | async-done | bytes 12582928 | tf_op jit(solution)/shard_map/all_gather | solution.py:15
  108.5 4.4 %fusion.3 = f32[256,1024]{1,0:T(8,128)} fusion(bf16[256,2048]{1,0:T(8,128)(2,1)S(1)} %bitcast.100, bf16[3,2048,1024]{2,1,0:T(8,128)(2,1)} %all-gather.2.cloned.1.call-done), kind=kOutput, calls=%fused_computation.10 | convolution fusion | flops 1073741824 | bytes 6291456 | tf_op jit(solution)/shard_map/dot_general | solution.py:71
  112.9 4.4 %fusion.1 = f32[256,1024]{1,0:T(8,128)} fusion(bf16[256,2048]{1,0:T(8,128)(2,1)S(1)} %bitcast.101, bf16[3,2048,1024]{2,1,0:T(8,128)(2,1)} %all-gather.2.cloned.1.call-done), kind=kOutput, calls=%fused_computation.8 | convolution fusion | flops 1073741824 | bytes 6291456 | tf_op jit(solution)/shard_map/dot_general | solution.py:70
  117.3 4.4 %multiply_convert_fusion = (bf16[256,1024]{1,0:T(8,128)(2,1)S(1)}, bf16[256,1024]{1,0:T(8,128)(2,1)S(1)}, bf16[256,1024]{1,0:T(8,128)(2,1)S(1)}) fusion(f32[256,1024]{1,0:T(8,128)} %fusion.1, f32[256,1024]{1,0:T(8,128)} %fusion.3, bf16[256,2048]{1,0:T(8,128)(2,1)S(1)} %bitcast.104, bf16[3,2048,1024]{2,1,0:T(8,128)(2,1)} %all-gather.2.cloned.1.call-done), kind=kOutput, calls=%fused_computation.36 | convolution fusion | flops 1077936128 | bytes 8912896 | tf_op jit(solution)/shard_map/dot_general | solution.py:80
  125.7 21.2 %pad_maximum_fusion = bf16[2048,3072]{0,1:T(8,128)(2,1)} fusion(bf16[2048,1024]{0,1:T(8,128)(2,1)S(1)} %convolution_convert_fusion, bf16[2048,1024]{0,1:T(8,128)(2,1)S(1)} %convolution_convert_fusion.1, bf16[2048,1024]{0,1:T(8,128)(2,1)S(1)} %convolution_convert_fusion.2), kind=kLoop, calls=%fused_computation | loop fusion | flops 37748736 | bytes 25165824 | tf_op jit(solution)/shard_map/concatenate | solution.py:148
  146.9 16.6 %copy.68 = bf16[2048,3072]{1,0:T(8,128)(2,1)} copy(bf16[2048,3072]{0,1:T(8,128)(2,1)} %pad_maximum_fusion) | data formatting | bytes 25165824
  164.6 4.6 %fusion.8 = bf16[256,2048]{1,0:T(8,128)(2,1)} fusion(bf16[256,1024]{1,0:T(8,128)(2,1)S(1)} %copy-done.8, bf16[3,2048,1024]{2,1,0:T(8,128)(2,1)} %all-gather.2.cloned.1.call-done), kind=kOutput, calls=%fused_computation.17 | convolution fusion | flops 1074266112 | bytes 5767168 | tf_op jit(solution)/shard_map/dot_general | solution.py:73
  169.2 6.1 %all-to-all-start.1 = ((bf16[8,32,2048]{2,1,0:T(8,128)(2,1)}), bf16[8,32,2048]{2,1,0:T(8,128)(2,1)S(1)}, u32[]{:S(2)}, u32[]{:S(2)}) async-start(bf16[8,32,2048]{2,1,0:T(8,128)(2,1)} %bitcast.8), calls=%async_computation.1 | async-start | bytes 2097152 | tf_op jit(solution)/shard_map/all_to_all | solution.py:121
  175.3 3.5 %fusion = f32[256,2048]{1,0:T(8,128)S(1)} fusion(bf16[256,1024]{1,0:T(8,128)(2,1)S(1)} %copy-done.6, bf16[3,2048,1024]{2,1,0:T(8,128)(2,1)} %all-gather.2.cloned.1.call-done), kind=kOutput, calls=%fused_computation.7 | convolution fusion | flops 1073741824 | bytes 6815744 | tf_op jit(solution)/shard_map/dot_general | solution.py:85
  178.9 4.5 %fusion.7 = bf16[256,2048]{1,0:T(8,128)(2,1)} fusion(f32[256,2048]{1,0:T(8,128)S(1)} %fusion, bf16[256,1024]{1,0:T(8,128)(2,1)S(1)} %copy-done.4, bf16[3,2048,1024]{2,1,0:T(8,128)(2,1)} %all-gather.2.cloned.1.call-done), kind=kOutput, calls=%fused_computation.16 | convolution fusion | flops 1074790400 | bytes 7864320 | tf_op jit(solution)/shard_map/dot_general | solution.py:87
  183.4 14.9 %all-to-all-done.1 = bf16[8,32,2048]{2,1,0:T(8,128)(2,1)S(1)} async-done(((bf16[8,32,2048]{2,1,0:T(8,128)(2,1)}), bf16[8,32,2048]{2,1,0:T(8,128)(2,1)S(1)}, u32[]{:S(2)}, u32[]{:S(2)}) %all-to-all-start.1) | async-done | bytes 1048608 | tf_op jit(solution)/shard_map/all_to_all | solution.py:121
  198.3 3.6 %all-to-all-start.3 = ((bf16[8,32,2048]{2,1,0:T(8,128)(2,1)}), bf16[8,32,2048]{2,1,0:T(8,128)(2,1)S(1)}, u32[]{:S(2)}, u32[]{:S(2)}) async-start(bf16[8,32,2048]{2,1,0:T(8,128)(2,1)} %bitcast.110), calls=%async_computation.3 | async-start | bytes 2097152 | tf_op jit(solution)/shard_map/all_to_all | solution.py:141
  202.4 3.6 %fusion.18 = f32[1,128,8]{2,0,1:T(1,128)S(1)} fusion(f32[256,1,1]{0,1,2:T(1,128)S(1)} %bitcast.115, s32[128,8]{1,0:T(8,128)S(1)} %copy.59), kind=kOutput, calls=%fused_computation.42 | convolution fusion | flops 3407872 | bytes 9216 | tf_op jit(solution)/shard_map/tks,s->tk/dot_general | solution.py:128
  207.6 16.8 %all-to-all-done.3 = bf16[8,32,2048]{2,1,0:T(8,128)(2,1)S(1)} async-done(((bf16[8,32,2048]{2,1,0:T(8,128)(2,1)}), bf16[8,32,2048]{2,1,0:T(8,128)(2,1)S(1)}, u32[]{:S(2)}, u32[]{:S(2)}) %all-to-all-start.3) | async-done | bytes 1048608 | tf_op jit(solution)/shard_map/all_to_all | solution.py:141
  224.4 6.8 %all-to-all-start.4 = ((bf16[16,128,64]{1,2,0:T(8,128)(2,1)}), bf16[16,128,64]{1,2,0:T(8,128)(2,1)S(1)}, u32[]{:S(2)}, u32[]{:S(2)}) async-start(bf16[16,128,64]{1,2,0:T(8,128)(2,1)} %bitcast.98), calls=%async_computation.4 | async-start | bytes 524288 | tf_op jit(solution)/shard_map/all_to_all | solution.py:30
  235.2 5.1 %all-to-all-done.4 = bf16[16,128,64]{1,2,0:T(8,128)(2,1)S(1)} async-done(((bf16[16,128,64]{1,2,0:T(8,128)(2,1)}), bf16[16,128,64]{1,2,0:T(8,128)(2,1)S(1)}, u32[]{:S(2)}, u32[]{:S(2)}) %all-to-all-start.4) | async-done | bytes 262176 | tf_op jit(solution)/shard_map/all_to_all | solution.py:30
  241.0 3.4 %all-to-all-start.5 = ((bf16[8,128,64]{1,2,0:T(8,128)(2,1)}), bf16[8,128,64]{1,2,0:T(8,128)(2,1)S(1)}, u32[]{:S(2)}, u32[]{:S(2)}) async-start(bf16[8,128,64]{1,2,0:T(8,128)(2,1)} %broadcast_in_dim.44), calls=%async_computation.5 | async-start | bytes 262144 | tf_op jit(solution)/shard_map/all_to_all | solution.py:36
  245.8 21.3 %psum.14 = f32[2048]{0:T(1024)S(1)} all-reduce(f32[2048]{0:T(1024)S(1)} %get-tuple-element.42), channel_id=1, replica_groups=mesh['dp'=16,'expert'=8] {'expert'}, use_global_device_ids=true, to_apply=%region_12.13 | all-reduce | flops 2048 | bytes 16384 | tf_op jit(solution)/shard_map/psum | solution.py:164
  267.1 32.5 %psum.15 = f32[2048]{0:T(1024)} all-reduce(f32[2048]{0:T(1024)S(1)} %psum.14), channel_id=1, replica_groups=mesh['dp'=16,'expert'=8] {'dp'}, use_global_device_ids=true, to_apply=%region_13.14 | all-reduce | flops 2048 | bytes 16384 | tf_op jit(solution)/shard_map/psum | solution.py:164
  (94 shorter events, 28.6 us)
Async XLA Ops:
  7.2 61.8 %copy-start = (bf16[128,2048]{1,0:T(8,128)(2,1)S(1)}, bf16[128,2048]{1,0:T(8,128)(2,1)}, u32[]{:S(2)}) copy-start(bf16[128,2048]{1,0:T(8,128)(2,1)} %param.15) | copy-start | bytes 1572868
  7.2 60.9 %copy-start.13 = (s32[128,8]{0,1:T(8,128)S(1)}, s32[128,8]{0,1:T(8,128)}, u32[]{:S(2)}) copy-start(s32[128,8]{0,1:T(8,128)} %param.11) | copy-start | bytes 12292
  7.2 60.5 %copy-start.1 = (bf16[128,2048]{1,0:T(8,128)(2,1)S(1)}, bf16[128,2048]{1,0:T(8,128)(2,1)}, u32[]{:S(2)}) copy-start(bf16[128,2048]{1,0:T(8,128)(2,1)} %param.8) | copy-start | bytes 1572868
  7.2 60.5 %copy-start.12 = (f32[2048]{0:T(1024)S(1)}, f32[2048]{0:T(1024)}, u32[]{:S(2)}) copy-start(f32[2048]{0:T(1024)} %param.9) | copy-start | bytes 24580
  7.2 18.7 %copy-start.14 = (bf16[128,64]{0,1:T(8,128)(2,1)S(1)}, bf16[128,64]{0,1:T(8,128)(2,1)}, u32[]{:S(2)}) copy-start(bf16[128,64]{0,1:T(8,128)(2,1)} %param.10) | copy-start | bytes 49156
  7.2 101.3 %all-gather.2.cloned.1.call-start = ((), (), s32[]{:S(2)}) async-start(), calls=%async_computation.7 | async-start | bytes 13369344 | tf_op jit(solution)/shard_map/all_gather | solution.py:15
  15.9 10.0 %copy-start.17 = (f32[128]{0:T(128)}, f32[128]{0:T(128)S(1)}, u32[]{:S(2)}) copy-start(f32[128]{0:T(128)S(1)} %fusion.16) | copy-start | bytes 1540
  15.9 190.3 %copy-start.15 = (f32[128]{0:T(128)}, f32[128]{0:T(128)S(1)}, u32[]{:S(2)}) copy-start(f32[128]{0:T(128)S(1)} %fusion.34) | copy-start | bytes 1540
  18.4 52.6 %all-to-all-start = ((bf16[8,32,2048]{2,1,0:T(8,128)(2,1)}), bf16[8,32,2048]{2,1,0:T(8,128)(2,1)S(1)}, u32[]{:S(2)}, u32[]{:S(2)}) async-start(bf16[8,32,2048]{2,1,0:T(8,128)(2,1)} %bitcast.3), calls=%async_computation | async-start | bytes 2097152 | tf_op jit(solution)/shard_map/all_to_all | solution.py:114
  69.0 2.1 copy-start.9
  71.1 46.3 %all-to-all-start.2 = ((bf16[8,32,2048]{2,1,0:T(8,128)(2,1)}), bf16[8,32,2048]{2,1,0:T(8,128)(2,1)S(1)}, u32[]{:S(2)}, u32[]{:S(2)}) async-start(bf16[8,32,2048]{2,1,0:T(8,128)(2,1)} %bitcast.109), calls=%async_computation.2 | async-start | bytes 2097152 | tf_op jit(solution)/shard_map/all_to_all | solution.py:135
  77.9 222.3 %reduce-scatter.4.cloned.1.call-start = ((), (), s32[]{:S(2)}) async-start(), calls=%async_computation.8 | async-start | bytes 13369344
  121.7 1.4 copy-start.7
  121.7 1.4 copy-start.3
  121.7 2.7 copy-start.5
  163.5 1.0 copy-start.8
  164.6 10.7 %copy-start.6 = (bf16[256,1024]{1,0:T(8,128)(2,1)S(1)}, bf16[256,1024]{1,0:T(8,128)(2,1)}, u32[]{:S(2)}) copy-start(bf16[256,1024]{1,0:T(8,128)(2,1)} %copy-done.5) | copy-start | bytes 1572868
  169.2 29.1 %all-to-all-start.1 = ((bf16[8,32,2048]{2,1,0:T(8,128)(2,1)}), bf16[8,32,2048]{2,1,0:T(8,128)(2,1)S(1)}, u32[]{:S(2)}, u32[]{:S(2)}) async-start(bf16[8,32,2048]{2,1,0:T(8,128)(2,1)} %bitcast.8), calls=%async_computation.1 | async-start | bytes 2097152 | tf_op jit(solution)/shard_map/all_to_all | solution.py:121
  175.3 3.5 %copy-start.4 = (bf16[256,1024]{1,0:T(8,128)(2,1)S(1)}, bf16[256,1024]{1,0:T(8,128)(2,1)}, u32[]{:S(2)}) copy-start(bf16[256,1024]{1,0:T(8,128)(2,1)} %copy-done.3) | copy-start | bytes 1572868
  198.3 26.1 %all-to-all-start.3 = ((bf16[8,32,2048]{2,1,0:T(8,128)(2,1)}), bf16[8,32,2048]{2,1,0:T(8,128)(2,1)S(1)}, u32[]{:S(2)}, u32[]{:S(2)}) async-start(bf16[8,32,2048]{2,1,0:T(8,128)(2,1)} %bitcast.110), calls=%async_computation.3 | async-start | bytes 2097152 | tf_op jit(solution)/shard_map/all_to_all | solution.py:141
  224.4 15.9 %all-to-all-start.4 = ((bf16[16,128,64]{1,2,0:T(8,128)(2,1)}), bf16[16,128,64]{1,2,0:T(8,128)(2,1)S(1)}, u32[]{:S(2)}, u32[]{:S(2)}) async-start(bf16[16,128,64]{1,2,0:T(8,128)(2,1)} %bitcast.98), calls=%async_computation.4 | async-start | bytes 524288 | tf_op jit(solution)/shard_map/all_to_all | solution.py:30
  231.2 2.9 copy-start.16
  231.5 12.9 %copy-start.10 = (f32[128,1,256]{2,1,0:T(1,128)S(1)}, f32[128,1,256]{2,1,0:T(1,128)}, u32[]{:S(2)}) copy-start(f32[128,1,256]{2,1,0:T(1,128)} %copy-done.9) | copy-start | bytes 393220
  241.0 58.6 %all-to-all-start.5 = ((bf16[8,128,64]{1,2,0:T(8,128)(2,1)}), bf16[8,128,64]{1,2,0:T(8,128)(2,1)S(1)}, u32[]{:S(2)}, u32[]{:S(2)}) async-start(bf16[8,128,64]{1,2,0:T(8,128)(2,1)} %broadcast_in_dim.44), calls=%async_computation.5 | async-start | bytes 262144 | tf_op jit(solution)/shard_map/all_to_all | solution.py:36
  (2 other events, 1.3 us)
Sparse Core Ops, SparseCore 0:
  9.7 98.7 all-gather.1
  163.7 107.3 reduce-scatter.3
